TPU v7x, 32 devices: a whole 2x2x4 slice. The times are simulated.
32 devices in a mesh: ep: 4 (over z), fsdp: 8 (over y, x, core).
Axes of the slice: x: 2, y: 2, z: 4, core: 2. Of those that a mesh axis runs over, the one named last changes fastest.
Arguments:
- train_gate: float32 [64, 2048, 1408], P('ep', 'fsdp'), may hold values from -0.1875 to 0.1875
- train_up: float32 [64, 2048, 1408], P('ep', 'fsdp'), may hold values from -0.1875 to 0.1875
- train_down: float32 [64, 1408, 2048], P('ep', None, 'fsdp'), may hold values from -0.21875 to 0.21875
- router_weight: float32 [2048, 64], P('fsdp', 'ep'), may hold values from -0.125 to 0.125
- router_gain: float32 [2048], P('fsdp'), may hold values from 0.25 to 1.75
Outputs:
- ready_gate: bfloat16 [64, 2048, 1408], P('ep', None, 'fsdp')
- ready_up: bfloat16 [64, 2048, 1408], P('ep', None, 'fsdp')
- ready_down: bfloat16 [64, 1408, 2048], P('ep', 'fsdp')
- scale_gate: float32 [64, 1408], P('ep', 'fsdp')
- scale_up: float32 [64, 1408], P('ep', 'fsdp')
- scale_down: float32 [64, 1408], P('ep', 'fsdp')
- serve_router: bfloat16 [2048, 64], replicated
All inputs are finite; a program needn't handle non-finite values.
Results may differ from a plain program's by a relative error of at most 0.001.
Values may be sent and summed in bfloat16 or wider, within the bound.
A program may use at most 192 MiB of HBM per device.

v0:
```python
import jax
import jax.numpy as jnp
from jax import lax
from jax.sharding import PartitionSpec as P


def body(train_gate, train_up, train_down, router_weight, router_gain):
    total_gate, total_up, total_down = lax.psum(
        (
            jnp.sum(train_gate * train_gate, axis=1),
            jnp.sum(train_up * train_up, axis=1),
            jnp.sum(train_down * train_down, axis=2),
        ),
        "fsdp",
    )
    scale_gate = jnp.sqrt(total_gate)
    scale_up = jnp.sqrt(total_up)
    scale_down = jnp.sqrt(total_down)
    narrow_gate, narrow_up, narrow_down = (
        (train_gate / jnp.expand_dims(scale_gate, 1)).astype(jnp.bfloat16),
        (train_up / jnp.expand_dims(scale_up, 1)).astype(jnp.bfloat16),
        (train_down / jnp.expand_dims(scale_down, 2)).astype(jnp.bfloat16),
    )
    ready_gate, ready_up = (
        lax.all_to_all(narrow_gate, "fsdp", split_axis=2, concat_axis=1, tiled=True),
        lax.all_to_all(narrow_up, "fsdp", split_axis=2, concat_axis=1, tiled=True),
    )
    ready_down = lax.all_to_all(narrow_down, "fsdp", split_axis=1, concat_axis=2, tiled=True)
    scale_gate = lax.dynamic_slice_in_dim(
        scale_gate, lax.axis_index("fsdp") * ready_gate.shape[2], ready_gate.shape[2], axis=1
    )
    scale_up = lax.dynamic_slice_in_dim(
        scale_up, lax.axis_index("fsdp") * ready_up.shape[2], ready_up.shape[2], axis=1
    )
    scale_down = lax.dynamic_slice_in_dim(
        scale_down, lax.axis_index("fsdp") * ready_down.shape[1], ready_down.shape[1], axis=1
    )
    part_router = (router_weight * router_gain[:, None]).astype(jnp.bfloat16)
    row_router = lax.all_gather(part_router, "fsdp", axis=0, tiled=True)
    serve_router = lax.all_gather(row_router, "ep", axis=1, tiled=True)
    return (ready_gate, ready_up, ready_down, scale_gate, scale_up, scale_down, serve_router)


def solution(mesh):
    return jax.shard_map(
        body,
        mesh=mesh,
        in_specs=(
            P("ep", "fsdp", None),
            P("ep", "fsdp", None),
            P("ep", None, "fsdp"),
            P("fsdp", "ep"),
            P("fsdp"),
        ),
        out_specs=(
            P("ep", None, "fsdp"),
            P("ep", None, "fsdp"),
            P("ep", "fsdp", None),
            P("ep", "fsdp"),
            P("ep", "fsdp"),
            P("ep", "fsdp"),
            P(),
        ),
        check_vma=False,
    )
```

profile of v0, /device:TPU:0, one launch (start us, length us, event | category | flops | bytes accessed | tf_op | source)
XLA Modules:
  0.0 618.1 jit_solution(2208627624309375978)
XLA Ops:
  7.2 0.0 all-reduce.3.cloned.1.call-start
  7.2 9.2 %multiply_reduce_fusion = f32[16,1408]{1,0:T(8,128)} fusion(f32[16,1408,256]{2,1,0:T(8,128)} %param.7), kind=kLoop, calls=%fused_computation.2 | loop fusion | flops 11511808 | bytes 23158784 | tf_op jit(solution)/shard_map/reduce_sum | solution.py:12
  16.4 5.0 copy-done
  21.4 11.0 %multiply_reduce_fusion.1 = (f32[16,1408]{1,0:T(8,128)}, f32[16,1408]{1,0:T(8,128)}) fusion(f32[16,256,1408]{2,1,0:T(8,128)S(1)} %copy-done, f32[16,256,1408]{2,1,0:T(8,128)} %param.5), kind=kLoop, calls=%fused_computation.4 | loop fusion | flops 23023616 | bytes 46317568 | tf_op jit(solution)/shard_map/reduce_sum | solution.py:11
  32.5 0.0 all-reduce.3.cloned.1.call-update
  32.5 23.7 %copy.28 = f32[16,256,1408]{1,0,2:T(8,128)} copy(f32[16,256,1408]{2,1,0:T(8,128)} %param.6) | data formatting | bytes 46137344 | tf_op args[1]
  56.2 32.6 %all-reduce.3.cloned.1.call-done = (f32[16,1408]{1,0:T(8,128)}, f32[16,1408]{1,0:T(8,128)}, f32[16,1408]{1,0:T(8,128)}) async-done(((f32[16,1408]{1,0:T(8,128)}, f32[16,1408]{1,0:T(8,128)}, f32[16,1408]{1,0:T(8,128)}), (f32[16,1408]{1,0:T(8,128)}, f32[16,1408]{1,0:T(8,128)}, f32[16,1408]{1,0:T(8,128)})) %all-reduce.3.cloned.1.call-update) | async-done | bytes 270352 | tf_op jit(solution)/shard_map/psum | solution.py:8
  88.8 0.9 sqrt.10
  89.7 0.3 copy.27
  90.0 14.2 %divide_convert_fusion = bf16[16,256,1408]{1,0,2:T(8,128)(2,1)} fusion(f32[16,256,1408]{1,0,2:T(8,128)} %copy.28, f32[16,1408]{0,1:T(8,128)S(1)} %copy.27), kind=kLoop, calls=%fused_computation.3 | loop fusion | flops 11534336 | bytes 34693120 | tf_op jit(solution)/shard_map/convert_element_type | solution.py:21
  104.2 5.2 all-to-all-start.1
  109.5 23.7 %copy.24 = f32[16,256,1408]{1,0,2:T(8,128)} copy(f32[16,256,1408]{2,1,0:T(8,128)} %param.5) | data formatting | bytes 46137344 | tf_op args[0]
  133.2 0.3 copy.23
  133.5 14.2 %divide_convert_fusion.1 = bf16[16,256,1408]{1,0,2:T(8,128)(2,1)} fusion(f32[16,256,1408]{1,0,2:T(8,128)} %copy.24, f32[16,1408]{0,1:T(8,128)S(1)} %copy.23), kind=kLoop, calls=%fused_computation.5 | loop fusion | flops 11534336 | bytes 34693120 | tf_op jit(solution)/shard_map/convert_element_type | solution.py:20
  147.7 89.5 %all-to-all-done.1 = bf16[16,256,1408]{1,0,2:T(8,128)(2,1)} async-done(((bf16[16,256,1408]{1,0,2:T(8,128)(2,1)}), bf16[16,256,1408]{1,0,2:T(8,128)(2,1)}, u32[]{:S(2)}, u32[]{:S(2)}) %all-to-all-start.1) | async-done | bytes 11534368 | tf_op jit(solution)/shard_map/all_to_all | solution.py:26
  237.2 5.3 all-to-all-start
  242.5 0.3 copy.31
  242.8 32.6 %fusion = bf16[16,1408,256]{2,0,1:T(8,128)(2,1)} fusion(f32[16,1408,256]{2,1,0:T(8,128)} %param.7, f32[16,1408]{0,1:T(8,128)S(1)} %copy.31), kind=kLoop, calls=%fused_computation.1 | loop fusion | flops 11534336 | bytes 34693120 | tf_op jit(solution)/shard_map/convert_element_type | solution.py:22
  275.4 94.8 %all-to-all-done = bf16[16,256,1408]{1,0,2:T(8,128)(2,1)} async-done(((bf16[16,256,1408]{1,0,2:T(8,128)(2,1)}), bf16[16,256,1408]{1,0,2:T(8,128)(2,1)}, u32[]{:S(2)}, u32[]{:S(2)}) %all-to-all-start) | async-done | bytes 11534368 | tf_op jit(solution)/shard_map/all_to_all | solution.py:25
  370.2 5.3 all-to-all-start.2
  375.5 130.9 %all_gather.6 = bf16[2048,16]{0,1:T(8,128)(2,1)S(1)} all-gather(bf16[256,16]{0,1:T(8,128)(2,1)S(1)} %multiply_convert_fusion), channel_id=1, replica_groups=mesh['ep'=4,'fsdp'=8] {'fsdp'}, dimensions={0}, use_global_device_ids=true | all-gather | bytes 73728 | tf_op jit(solution)/shard_map/all_gather | solution.py:39
  506.4 14.2 %all_gather.7 = bf16[2048,64]{0,1:T(8,128)(2,1)S(1)} all-gather(bf16[2048,16]{0,1:T(8,128)(2,1)S(1)} %all_gather.6), channel_id=1, replica_groups=mesh['ep'=4,'fsdp'=8] {'ep'}, dimensions={1}, use_global_device_ids=true | all-gather | bytes 327680 | tf_op jit(solution)/shard_map/all_gather | solution.py:40
  520.6 0.7 constant_dynamic-slice_fusion
  521.3 0.7 constant_dynamic-slice_fusion.1
  522.0 0.7 constant_dynamic-slice_fusion.2
  522.6 11.3 %copy.30 = bf16[16,8,256,176]{2,1,3,0:T(8,128)(2,1)} copy(bf16[16,8,256,176]{2,0,3,1:T(8,128)(2,1)} %bitcast.5) | data formatting | bytes 23068672 | tf_op jit(solution)/shard_map/all_to_all | solution.py:26
  534.0 18.0 %all_to_all.46 = bf16[16,2048,176]{1,2,0:T(8,128)(2,1)} reshape(bf16[16,8,256,176]{2,1,3,0:T(8,128)(2,1)} %copy.30) | data formatting | bytes 23068672 | tf_op jit(solution)/shard_map/all_to_all | solution.py:26
  551.9 11.3 %copy.26 = bf16[16,8,256,176]{2,1,3,0:T(8,128)(2,1)} copy(bf16[16,8,256,176]{2,0,3,1:T(8,128)(2,1)} %bitcast.2) | data formatting | bytes 23068672 | tf_op jit(solution)/shard_map/all_to_all | solution.py:25
  563.3 18.0 %all_to_all.42 = bf16[16,2048,176]{1,2,0:T(8,128)(2,1)} reshape(bf16[16,8,256,176]{2,1,3,0:T(8,128)(2,1)} %copy.26) | data formatting | bytes 23068672 | tf_op jit(solution)/shard_map/all_to_all | solution.py:25
  581.2 11.3 %copy.33 = bf16[16,176,8,256]{3,2,1,0:T(8,128)(2,1)} copy(bf16[16,176,8,256]{3,0,1,2:T(8,128)(2,1)} %bitcast.7) | data formatting | bytes 23068672 | tf_op jit(solution)/shard_map/all_to_all | solution.py:28
  592.5 18.0 %all_to_all.50 = bf16[16,176,2048]{2,1,0:T(8,128)(2,1)} reshape(bf16[16,176,8,256]{3,2,1,0:T(8,128)(2,1)} %copy.33) | data formatting | bytes 23068672 | tf_op jit(solution)/shard_map/all_to_all | solution.py:28
  610.5 0.7 copy.43
  (13 shorter events, 0.1 us)
Async XLA Ops:
  7.2 81.6 %all-reduce.3.cloned.1.call-start = ((), (), s32[]{:S(2)}) async-start(), calls=%async_computation.3 | async-start | bytes 540672 | tf_op jit(solution)/shard_map/psum | solution.py:8
  7.2 14.2 %copy-start = (f32[16,256,1408]{2,1,0:T(8,128)S(1)}, f32[16,256,1408]{2,1,0:T(8,128)}, u32[]{:S(2)}) copy-start(f32[16,256,1408]{2,1,0:T(8,128)} %param.6) | copy-start | bytes 69206016
  104.2 133.0 %all-to-all-start.1 = ((bf16[16,256,1408]{1,0,2:T(8,128)(2,1)}), bf16[16,256,1408]{1,0,2:T(8,128)(2,1)}, u32[]{:S(2)}, u32[]{:S(2)}) async-start(bf16[16,256,1408]{1,0,2:T(8,128)(2,1)} %divide_convert_fusion), calls=%async_computation.1 | async-start | bytes 23068672 | tf_op jit(solution)/shard_map/all_to_all | solution.py:26
  109.5 23.7 %copy-start.2 = (f32[16,1408]{1,0:T(8,128)S(1)}, f32[16,1408]{1,0:T(8,128)}, u32[]{:S(2)}) copy-start(f32[16,1408]{1,0:T(8,128)} %get-tuple-element.7) | copy-start | bytes 270340
  133.5 109.0 %copy-start.1 = (f32[16,1408]{1,0:T(8,128)S(1)}, f32[16,1408]{1,0:T(8,128)}, u32[]{:S(2)}) copy-start(f32[16,1408]{1,0:T(8,128)} %get-tuple-element.9) | copy-start | bytes 270340
  237.2 133.0 %all-to-all-start = ((bf16[16,256,1408]{1,0,2:T(8,128)(2,1)}), bf16[16,256,1408]{1,0,2:T(8,128)(2,1)}, u32[]{:S(2)}, u32[]{:S(2)}) async-start(bf16[16,256,1408]{1,0,2:T(8,128)(2,1)} %divide_convert_fusion.1), calls=%async_computation | async-start | bytes 23068672 | tf_op jit(solution)/shard_map/all_to_all | solution.py:25
  242.8 132.7 %copy-start.3 = (f32[256,16]{0,1:T(8,128)S(1)}, f32[256,16]{0,1:T(8,128)}, u32[]{:S(2)}) copy-start(f32[256,16]{0,1:T(8,128)} %param.8) | copy-start | bytes 49156
  242.8 132.7 %copy-start.4 = (f32[256]{0:T(256)S(1)}, f32[256]{0:T(256)}, u32[]{:S(2)}) copy-start(f32[256]{0:T(256)} %param.9) | copy-start | bytes 3076
  370.2 211.0 %all-to-all-start.2 = ((bf16[16,1408,256]{2,0,1:T(8,128)(2,1)}), bf16[16,1408,256]{2,0,1:T(8,128)(2,1)}, u32[]{:S(2)}, u32[]{:S(2)}) async-start(bf16[16,1408,256]{2,0,1:T(8,128)(2,1)} %fusion), calls=%async_computation.2 | async-start | bytes 23068672 | tf_op jit(solution)/shard_map/all_to_all | solution.py:28
Sparse Core Ops, SparseCore 0:
  32.6 56.1 all-reduce.2
where the time goes:
time: 621 us; the launch traced here: 618 us
  waiting for transfers between devices  217 us (35%)
  local copies, waits for them, and re-layouts  145 us (23%)
  blocking collectives  145 us (23%)
  other arithmetic  81.3 us (13%)
  starting transfers between devices  15.8 us (3%)
  between operations  14.2 us (2%)
    all_gather x1, blocking collectives, body(): row_router = lax.all_gather(part_router, 'fsdp', axis=0, tiled=True)  131 us
    all_to_all x1, waiting for transfers between devices, body(): lax.all_to_all(narrow_gate, 'fsdp', split_axis=2, concat_axis=1, tiled=True)  94.8 us
    all_to_all x1, waiting for transfers between devices, body(): lax.all_to_all(narrow_up, 'fsdp', split_axis=2, concat_axis=1, tiled=True)  89.5 us
    unnamed x13, local copies, waits for them, and re-layouts  53.2 us
    psum x1, waiting for transfers between devices, body(): lax.psum((jnp.sum(train_gate * train_gate, axis=1), jnp.sum(train_up * tr...  32.6 us
    convert_element_type x1, other arithmetic, body(): (train_down / jnp.expand_dims(scale_down, 2)).astype(jnp.bfloat16)  32.6 us
    all_to_all x2, local copies, waits for them, and re-layouts, body(): lax.all_to_all(narrow_up, 'fsdp', split_axis=2, concat_axis=1, tiled=True)  29.3 us
    all_to_all x2, local copies, waits for them, and re-layouts, body(): lax.all_to_all(narrow_gate, 'fsdp', split_axis=2, concat_axis=1, tiled=True)  29.3 us
  transfers between devices with their start and end apart: 4, of which 3 were waited for; matrix products, arithmetic and copies ran while one was open for 19% of the time, Pallas kernels for 0%

commit v1 on v0

--- a/solution.py
+++ b/solution.py
@@ -36,7 +36,13 @@
         scale_down, lax.axis_index("fsdp") * ready_down.shape[1], ready_down.shape[1], axis=1
     )
     part_router = (router_weight * router_gain[:, None]).astype(jnp.bfloat16)
-    row_router = lax.all_gather(part_router, "fsdp", axis=0, tiled=True)
+    peers = lax.axis_size("fsdp")
+    held, parts = (part_router, [part_router])
+    for _ in range(peers - 1):
+        held = lax.ppermute(held, "fsdp", [(i, (i + 1) % peers) for i in range(peers)])
+        parts.insert(0, held)
+    line = jnp.concatenate(parts, axis=0)
+    row_router = jnp.roll(line, (lax.axis_index("fsdp") + 1) * part_router.shape[0], axis=0)
     serve_router = lax.all_gather(row_router, "ep", axis=1, tiled=True)
     return (ready_gate, ready_up, ready_down, scale_gate, scale_up, scale_down, serve_router)
 

time: 621 us -> 642 us (1.034)
  waiting for transfers between devices: 217 us -> 368 us
  blocking collectives: 145 us -> 14.6 us
    ppermute x0 -> x7, waiting for transfers between devices: none -> 151 us  [body(): lax.ppermute(held, 'fsdp', [(i, (i + 1) % peers) for i in range(peers)])]
    all_gather x1 -> x0, blocking collectives: 131 us -> none  [body(): row_router = lax.all_gather(part_router, 'fsdp', axis=0, tiled=True)]
    unnamed x13 -> x27, local copies, waits for them, and re-layouts: 53.2 us -> 53.2 us
  transfers between devices with their start and end apart: 4 -> 11, of which waited for: 3 -> 10; matrix products, arithmetic and copies ran while one was open for 19% -> 19% of each run, Pallas kernels for 0% -> 0%
where the time goes in v1:
time: 642 us; the launch traced here: 639 us
  waiting for transfers between devices  368 us (57%)
  local copies, waits for them, and re-layouts  145 us (23%)
  other arithmetic  81.2 us (13%)
  starting transfers between devices  16.2 us (3%)
  blocking collectives  14.6 us (2%)
  between operations  14.3 us (2%)
    ppermute x7, waiting for transfers between devices, body(): lax.ppermute(held, 'fsdp', [(i, (i + 1) % peers) for i in range(peers)])  151 us
    all_to_all x1, waiting for transfers between devices, body(): lax.all_to_all(narrow_up, 'fsdp', split_axis=2, concat_axis=1, tiled=True)  94.8 us
    all_to_all x1, waiting for transfers between devices, body(): lax.all_to_all(narrow_gate, 'fsdp', split_axis=2, concat_axis=1, tiled=True)  89.5 us
    unnamed x27, local copies, waits for them, and re-layouts  53.2 us
    psum x1, waiting for transfers between devices, body(): lax.psum((jnp.sum(train_gate * train_gate, axis=1), jnp.sum(train_up * tr...  32.6 us
    convert_element_type x1, other arithmetic, body(): (train_down / jnp.expand_dims(scale_down, 2)).astype(jnp.bfloat16)  32.6 us
    all_to_all x2, local copies, waits for them, and re-layouts, body(): lax.all_to_all(narrow_down, 'fsdp', split_axis=1, concat_axis=2, tiled=True)  29.4 us
    all_to_all x2, local copies, waits for them, and re-layouts, body(): lax.all_to_all(narrow_gate, 'fsdp', split_axis=2, concat_axis=1, tiled=True)  29.3 us
  transfers between devices with their start and end apart: 11, of which 10 were waited for; matrix products, arithmetic and copies ran while one was open for 19% of the time, Pallas kernels for 0%

profile of v1, /device:TPU:0, one launch (start us, length us, event | category | flops | bytes accessed | tf_op | source)
XLA Modules:
  0.0 638.9 jit_solution(10881935652031790808)
XLA Ops:
  7.2 9.2 %multiply_reduce_fusion = f32[16,1408]{1,0:T(8,128)} fusion(f32[16,1408,256]{2,1,0:T(8,128)} %param.7), kind=kLoop, calls=%fused_computation.2 | loop fusion | flops 11511808 | bytes 23158784 | tf_op jit(solution)/shard_map/reduce_sum | solution.py:12
  16.4 5.0 copy-done
  21.4 11.0 %multiply_reduce_fusion.1 = (f32[16,1408]{1,0:T(8,128)}, f32[16,1408]{1,0:T(8,128)}) fusion(f32[16,256,1408]{2,1,0:T(8,128)} %param.6, f32[16,256,1408]{2,1,0:T(8,128)S(1)} %copy-done), kind=kLoop, calls=%fused_computation.4 | loop fusion | flops 23023616 | bytes 46317568 | tf_op jit(solution)/shard_map/reduce_sum | solution.py:11
  32.5 23.7 %copy.24 = f32[16,256,1408]{1,0,2:T(8,128)} copy(f32[16,256,1408]{2,1,0:T(8,128)} %param.5) | data formatting | bytes 46137344 | tf_op args[0]
  56.2 32.6 %all-reduce.3.cloned.1.call-done = (f32[16,1408]{1,0:T(8,128)}, f32[16,1408]{1,0:T(8,128)}, f32[16,1408]{1,0:T(8,128)}) async-done(((f32[16,1408]{1,0:T(8,128)}, f32[16,1408]{1,0:T(8,128)}, f32[16,1408]{1,0:T(8,128)}), (f32[16,1408]{1,0:T(8,128)}, f32[16,1408]{1,0:T(8,128)}, f32[16,1408]{1,0:T(8,128)})) %all-reduce.3.cloned.1.call-update) | async-done | bytes 270352 | tf_op jit(solution)/shard_map/psum | solution.py:8
  88.8 0.9 sqrt.9
  90.0 14.2 %divide_convert_fusion.1 = bf16[16,256,1408]{1,0,2:T(8,128)(2,1)} fusion(f32[16,256,1408]{1,0,2:T(8,128)} %copy.24, f32[16,1408]{0,1:T(8,128)S(1)} %copy.23), kind=kLoop, calls=%fused_computation.5 | loop fusion | flops 11534336 | bytes 34693120 | tf_op jit(solution)/shard_map/convert_element_type | solution.py:20
  104.2 5.2 all-to-all-start
  109.4 23.7 %copy.28 = f32[16,256,1408]{1,0,2:T(8,128)} copy(f32[16,256,1408]{2,1,0:T(8,128)} %param.6) | data formatting | bytes 46137344 | tf_op args[1]
  133.4 14.2 %divide_convert_fusion = bf16[16,256,1408]{1,0,2:T(8,128)(2,1)} fusion(f32[16,256,1408]{1,0,2:T(8,128)} %copy.28, f32[16,1408]{0,1:T(8,128)S(1)} %copy.27), kind=kLoop, calls=%fused_computation.3 | loop fusion | flops 11534336 | bytes 34693120 | tf_op jit(solution)/shard_map/convert_element_type | solution.py:21
  147.7 89.5 %all-to-all-done = bf16[16,256,1408]{1,0,2:T(8,128)(2,1)} async-done(((bf16[16,256,1408]{1,0,2:T(8,128)(2,1)}), bf16[16,256,1408]{1,0,2:T(8,128)(2,1)}, u32[]{:S(2)}, u32[]{:S(2)}) %all-to-all-start) | async-done | bytes 11534368 | tf_op jit(solution)/shard_map/all_to_all | solution.py:25
  237.2 5.3 all-to-all-start.1
  242.8 32.6 %fusion = bf16[16,1408,256]{2,0,1:T(8,128)(2,1)} fusion(f32[16,1408,256]{2,1,0:T(8,128)} %param.7, f32[16,1408]{0,1:T(8,128)S(1)} %copy.31), kind=kLoop, calls=%fused_computation.1 | loop fusion | flops 11534336 | bytes 34693120 | tf_op jit(solution)/shard_map/convert_element_type | solution.py:22
  275.4 94.8 %all-to-all-done.1 = bf16[16,256,1408]{1,0,2:T(8,128)(2,1)} async-done(((bf16[16,256,1408]{1,0,2:T(8,128)(2,1)}), bf16[16,256,1408]{1,0,2:T(8,128)(2,1)}, u32[]{:S(2)}, u32[]{:S(2)}) %all-to-all-start.1) | async-done | bytes 11534368 | tf_op jit(solution)/shard_map/all_to_all | solution.py:26
  370.2 5.3 all-to-all-start.2
  375.9 126.8 %collective-permute-done = bf16[256,16]{0,1:T(8,128)(2,1)S(1)} collective-permute-done((bf16[256,16]{0,1:T(8,128)(2,1)S(1)}, bf16[256,16]{0,1:T(8,128)(2,1)S(1)}, u32[]{:S(2)}, u32[]{:S(2)}) %collective-permute-start) | collective-permute-done | bytes 8224 | tf_op jit(solution)/shard_map/ppermute | solution.py:42
  502.7 4.0 collective-permute-done.1
  506.7 4.0 collective-permute-done.2
  510.7 4.0 collective-permute-done.3
  514.6 4.0 collective-permute-done.4
  518.6 4.0 collective-permute-done.5
  522.6 4.0 collective-permute-done.6
  526.7 14.6 %all_gather.3 = bf16[2048,64]{0,1:T(8,128)(2,1)S(1)} all-gather(bf16[2048,16]{0,1:T(8,128)(2,1)S(1)} %constant_dynamic-slice_fusion), channel_id=1, replica_groups=mesh['ep'=4,'fsdp'=8] {'ep'}, dimensions={1}, use_global_device_ids=true | all-gather | bytes 327680 | tf_op jit(solution)/shard_map/all_gather | solution.py:46
  541.3 0.7 constant_dynamic-slice_fusion.3
  542.0 0.7 constant_dynamic-slice_fusion.2
  543.3 11.3 %copy.26 = bf16[16,8,256,176]{2,1,3,0:T(8,128)(2,1)} copy(bf16[16,8,256,176]{2,0,3,1:T(8,128)(2,1)} %bitcast.2) | data formatting | bytes 23068672 | tf_op jit(solution)/shard_map/all_to_all | solution.py:25
  554.7 18.0 %all_to_all.42 = bf16[16,2048,176]{1,2,0:T(8,128)(2,1)} reshape(bf16[16,8,256,176]{2,1,3,0:T(8,128)(2,1)} %copy.26) | data formatting | bytes 23068672 | tf_op jit(solution)/shard_map/all_to_all | solution.py:25
  572.6 11.3 %copy.30 = bf16[16,8,256,176]{2,1,3,0:T(8,128)(2,1)} copy(bf16[16,8,256,176]{2,0,3,1:T(8,128)(2,1)} %bitcast.5) | data formatting | bytes 23068672 | tf_op jit(solution)/shard_map/all_to_all | solution.py:26
  584.0 18.0 %all_to_all.46 = bf16[16,2048,176]{1,2,0:T(8,128)(2,1)} reshape(bf16[16,8,256,176]{2,1,3,0:T(8,128)(2,1)} %copy.30) | data formatting | bytes 23068672 | tf_op jit(solution)/shard_map/all_to_all | solution.py:26
  601.9 11.4 %copy.33 = bf16[16,176,8,256]{3,2,1,0:T(8,128)(2,1)} copy(bf16[16,176,8,256]{3,0,1,2:T(8,128)(2,1)} %bitcast.7) | data formatting | bytes 23068672 | tf_op jit(solution)/shard_map/all_to_all | solution.py:28
  613.3 18.0 %all_to_all.50 = bf16[16,176,2048]{2,1,0:T(8,128)(2,1)} reshape(bf16[16,176,8,256]{3,2,1,0:T(8,128)(2,1)} %copy.33) | data formatting | bytes 23068672 | tf_op jit(solution)/shard_map/all_to_all | solution.py:28
  631.3 0.7 copy.58
  (43 shorter events, 2.1 us)
Async XLA Ops:
  7.2 81.6 %all-reduce.3.cloned.1.call-start = ((), (), s32[]{:S(2)}) async-start(), calls=%async_computation.3 | async-start | bytes 540672 | tf_op jit(solution)/shard_map/psum | solution.py:8
  7.2 14.2 %copy-start = (f32[16,256,1408]{2,1,0:T(8,128)S(1)}, f32[16,256,1408]{2,1,0:T(8,128)}, u32[]{:S(2)}) copy-start(f32[16,256,1408]{2,1,0:T(8,128)} %param.5) | copy-start | bytes 69206016
  104.2 133.0 %all-to-all-start = ((bf16[16,256,1408]{1,0,2:T(8,128)(2,1)}), bf16[16,256,1408]{1,0,2:T(8,128)(2,1)}, u32[]{:S(2)}, u32[]{:S(2)}) async-start(bf16[16,256,1408]{1,0,2:T(8,128)(2,1)} %divide_convert_fusion.1), calls=%async_computation | async-start | bytes 23068672 | tf_op jit(solution)/shard_map/all_to_all | solution.py:25
  109.4 23.7 %copy-start.3 = (f32[16,1408]{1,0:T(8,128)S(1)}, f32[16,1408]{1,0:T(8,128)}, u32[]{:S(2)}) copy-start(f32[16,1408]{1,0:T(8,128)} %get-tuple-element.8) | copy-start | bytes 270340
  133.4 109.0 %copy-start.2 = (f32[16,1408]{1,0:T(8,128)S(1)}, f32[16,1408]{1,0:T(8,128)}, u32[]{:S(2)}) copy-start(f32[16,1408]{1,0:T(8,128)} %get-tuple-element.9) | copy-start | bytes 270340
  237.2 133.0 %all-to-all-start.1 = ((bf16[16,256,1408]{1,0,2:T(8,128)(2,1)}), bf16[16,256,1408]{1,0,2:T(8,128)(2,1)}, u32[]{:S(2)}, u32[]{:S(2)}) async-start(bf16[16,256,1408]{1,0,2:T(8,128)(2,1)} %divide_convert_fusion), calls=%async_computation.1 | async-start | bytes 23068672 | tf_op jit(solution)/shard_map/all_to_all | solution.py:26
  242.7 132.7 %copy-start.1 = (f32[256,16]{0,1:T(8,128)S(1)}, f32[256,16]{0,1:T(8,128)}, u32[]{:S(2)}) copy-start(f32[256,16]{0,1:T(8,128)} %param.8) | copy-start | bytes 49156
  242.7 132.7 %copy-start.4 = (f32[256]{0:T(256)S(1)}, f32[256]{0:T(256)}, u32[]{:S(2)}) copy-start(f32[256]{0:T(256)} %param.9) | copy-start | bytes 3076
  370.2 231.8 %all-to-all-start.2 = ((bf16[16,1408,256]{2,0,1:T(8,128)(2,1)}), bf16[16,1408,256]{2,0,1:T(8,128)(2,1)}, u32[]{:S(2)}, u32[]{:S(2)}) async-start(bf16[16,1408,256]{2,0,1:T(8,128)(2,1)} %fusion), calls=%async_computation.2 | async-start | bytes 23068672 | tf_op jit(solution)/shard_map/all_to_all | solution.py:28
  375.5 127.2 %collective-permute-start = (bf16[256,16]{0,1:T(8,128)(2,1)S(1)}, bf16[256,16]{0,1:T(8,128)(2,1)S(1)}, u32[]{:S(2)}, u32[]{:S(2)}) collective-permute-start(bf16[256,16]{0,1:T(8,128)(2,1)S(1)} %multiply_convert_fusion), channel_id=1, source_target_pairs={{0,1},{1,2},{2,3},{3,4},{4,5},{5,6},{6,7},{7,0},{8,9},{9,10},{10,1... | collective-permute-start | bytes 24584 | tf_op jit(solution)/shard_map/ppermute | solution.py:42
  502.7 4.0 collective-permute-start.1
  506.7 4.0 collective-permute-start.2
  510.7 4.0 collective-permute-start.3
  514.6 4.0 collective-permute-start.4
  518.6 4.0 collective-permute-start.5
  522.6 4.0 collective-permute-start.6
Sparse Core Ops, SparseCore 0:
  32.6 56.1 all-reduce.2
